TPU v7x, 32 devices: a whole 2x2x4 slice. The times are simulated.
32 devices in a mesh: zero: 4 (over z), model: 4 (over x, core), trial: 2 (over y).
Axes of the slice: x: 2, y: 2, z: 4, core: 2. Of those that a mesh axis runs over, the one named last changes fastest.
Arguments:
- w_query: bfloat16 [4096, 2048], P(('trial', 'zero'), 'model'), parts along dimension 0, may hold values from -0.125 to 0.125
- low_query: bfloat16 [4096, 32], P(('trial', 'zero')), parts along dimension 0, may hold values from -0.125 to 0.125
- high_query: bfloat16 [64, 2048], P('trial', 'model'), parts along dimension 0, may hold values from -1 to 1
- w_key: bfloat16 [4096, 512], P(('trial', 'zero'), 'model'), parts along dimension 0, may hold values from -0.125 to 0.125
- low_key: bfloat16 [4096, 32], P(('trial', 'zero')), parts along dimension 0, may hold values from -0.125 to 0.125
- high_key: bfloat16 [64, 512], P('trial', 'model'), parts along dimension 0, may hold values from -1 to 1
- w_value: bfloat16 [4096, 512], P(('trial', 'zero'), 'model'), parts along dimension 0, may hold values from -0.125 to 0.125
- low_value: bfloat16 [4096, 32], P(('trial', 'zero')), parts along dimension 0, may hold values from -0.125 to 0.125
- high_value: bfloat16 [64, 512], P('trial', 'model'), parts along dimension 0, may hold values from -1 to 1
- w_mixed: bfloat16 [4096, 2048], P(('trial', 'model'), 'zero'), parts along dimension 0, may hold values from -0.125 to 0.125
- low_mixed: bfloat16 [4096, 32], P(('trial', 'model')), parts along dimension 0, may hold values from -0.125 to 0.125
- high_mixed: bfloat16 [64, 2048], P('trial', 'zero'), parts along dimension 0, may hold values from -1 to 1
- norm_train: float32 [4096], P(('trial', 'zero', 'model')), parts along dimension 0, may hold values from 0.25 to 1.75
- norm_step: float32 [4096], P(('trial', 'zero', 'model')), parts along dimension 0, may hold values from -0.3 to 0.3
Outputs:
- final_query: bfloat16 [4096, 2048], P('trial', 'model'), parts along dimension 0
- final_key: bfloat16 [4096, 512], P('trial', 'model'), parts along dimension 0
- final_value: bfloat16 [4096, 512], P('trial', 'model'), parts along dimension 0
- final_mixed: bfloat16 [4096, 2048], P(('trial', 'model')), parts along dimension 0
- serve_norm: bfloat16 [4096], P('trial'), parts along dimension 0
There are 2 independent parts, one for each index of `trial`. A program takes and returns all parts, laid end to end along the dimension named above; each array names one. Nothing has to cross between parts.
All inputs are finite; a program needn't handle non-finite values.
Results may differ from a plain program's by a relative error of at most 0.001.
Values may be sent and summed in bfloat16 or wider, within the bound.
A program may use at most 64 MiB of HBM per device.

v0:
```python
import jax
import jax.numpy as jnp
from jax import lax
from jax.sharding import PartitionSpec as P

mix_rate = 2.0


def shards(
    w_query,
    low_query,
    high_query,
    w_key,
    low_key,
    high_key,
    w_value,
    low_value,
    high_value,
    w_mixed,
    low_mixed,
    high_mixed,
    norm_train,
    norm_step,
):
    result_query = w_query.astype(jnp.float32) + mix_rate * jnp.dot(
        low_query, high_query, preferred_element_type=jnp.float32
    )
    result_key = w_key.astype(jnp.float32) + mix_rate * jnp.dot(
        low_key, high_key, preferred_element_type=jnp.float32
    )
    result_value = w_value.astype(jnp.float32) + mix_rate * jnp.dot(
        low_value, high_value, preferred_element_type=jnp.float32
    )
    result_mixed = w_mixed.astype(jnp.float32) + mix_rate * jnp.dot(
        low_mixed, high_mixed, preferred_element_type=jnp.float32
    )
    narrow_query, narrow_key, narrow_value, narrow_mixed = (
        result_query.astype(jnp.bfloat16),
        result_key.astype(jnp.bfloat16),
        result_value.astype(jnp.bfloat16),
        result_mixed.astype(jnp.bfloat16),
    )
    final_query, final_key, final_value, final_mixed = (
        lax.all_gather(narrow_query, "zero", axis=0, tiled=True),
        lax.all_gather(narrow_key, "zero", axis=0, tiled=True),
        lax.all_gather(narrow_value, "zero", axis=0, tiled=True),
        lax.all_gather(narrow_mixed, "zero", axis=1, tiled=True),
    )
    serve_norm = lax.all_gather(
        (norm_train + norm_step).astype(jnp.bfloat16), ("zero", "model"), axis=0, tiled=True
    )
    return (final_query, final_key, final_value, final_mixed, serve_norm)


def solution(mesh):
    placed = (
        P(("trial", "zero"), "model"),
        P(("trial", "zero"), None),
        P("trial", "model"),
        P(("trial", "zero"), "model"),
        P(("trial", "zero"), None),
        P("trial", "model"),
        P(("trial", "zero"), "model"),
        P(("trial", "zero"), None),
        P("trial", "model"),
        P(("trial", "model"), "zero"),
        P(("trial", "model"), None),
        P("trial", "zero"),
        P(("trial", "zero", "model")),
        P(("trial", "zero", "model")),
    )
    return jax.shard_map(
        shards,
        mesh=mesh,
        in_specs=placed,
        out_specs=(
            P("trial", "model"),
            P("trial", "model"),
            P("trial", "model"),
            P(("trial", "model"), None),
            P("trial"),
        ),
        check_vma=False,
    )
```

profile of v0, /device:TPU:0, one launch (start us, length us, event | category | flops | bytes accessed | tf_op | source)
XLA Modules:
  0.0 131.7 jit_solution(212639038545267897)
XLA Ops:
  7.2 0.0 copy-start
  7.2 0.0 copy-start.2
  7.2 0.0 copy-start.4
  7.2 0.0 copy-start.6
  7.2 0.0 copy-start.3
  7.2 0.0 copy-start.5
  7.2 0.0 copy-start.7
  7.2 0.0 all-gather.4.cloned.1.call-start
  7.3 0.6 copy-done
  7.9 2.2 %fusion.2 = bf16[512,512]{1,0:T(8,128)(2,1)} fusion(bf16[512,32]{0,1:T(8,128)(2,1)S(1)} %copy-done, bf16[32,512]{1,0:T(8,128)(2,1)} %param.16, bf16[512,512]{1,0:T(8,128)(2,1)} %param.14), kind=kOutput, calls=%fused_computation.4 | convolution fusion | flops 17825792 | bytes 1114112 | tf_op jit(solution)/shard_map/dot_general | solution.py:25
  10.1 0.0 copy-start.8
  10.1 0.0 copy-start.9
  10.1 0.0 all-gather.4.cloned.1.call-update
  10.1 0.0 all-gather.6.cloned.1.call-start
  10.2 2.2 %fusion.3 = bf16[512,512]{1,0:T(8,128)(2,1)} fusion(bf16[512,32]{0,1:T(8,128)(2,1)} %param.24, bf16[32,512]{1,0:T(8,128)(2,1)} %param.25, bf16[512,512]{1,0:T(8,128)(2,1)} %param.23), kind=kOutput, calls=%fused_computation.5 | convolution fusion | flops 17825792 | bytes 1114112 | tf_op jit(solution)/shard_map/dot_general | solution.py:34
  12.4 0.0 all-gather.6.cloned.1.call-update
  12.4 0.0 copy-done.2
  12.4 0.0 copy-done.4
  12.4 0.0 copy-done.6
  12.4 0.2 fusion.6
  12.7 23.1 %all_gather.16 = bf16[2048,128]{1,0:T(8,128)(2,1)S(1)} all-gather(bf16[512,128]{1,0:T(8,128)(2,1)S(1)} %fusion.6), channel_id=1, replica_groups=mesh['zero'=4,'model'=4,'trial'=2] {'zero'}, dimensions={0}, use_global_device_ids=true | all-gather | bytes 655360 | tf_op jit(solution)/shard_map/all_gather | solution.py:45
  35.8 0.0 copy-done.3
  35.8 0.0 copy-done.5
  35.8 0.0 copy-done.7
  35.8 0.2 fusion.7
  36.0 21.4 %all_gather.17 = bf16[2048,128]{1,0:T(8,128)(2,1)S(1)} all-gather(bf16[512,128]{1,0:T(8,128)(2,1)S(1)} %fusion.7), channel_id=1, replica_groups=mesh['zero'=4,'model'=4,'trial'=2] {'zero'}, dimensions={0}, use_global_device_ids=true | all-gather | bytes 655360 | tf_op jit(solution)/shard_map/all_gather | solution.py:46
  57.4 0.0 copy-done.8
  57.4 0.0 copy-done.9
  57.4 20.5 %all-gather = bf16[16,1,128]{2,1,0:T(2,128)(2,1)S(1)} all-gather(bf16[1,1,128]{2,1,0:T(2,128)(2,1)S(1)} %convert_bitcast_fusion), channel_id=1, replica_groups=mesh['zero'=4,'model'=4,'trial'=2] {'zero','model'}, dimensions={0}, use_global_device_ids=true | all-gather | bytes 4352 | tf_op jit(solution)/shard_map/all_gather | solution.py:49
  77.9 0.6 reduce
  78.5 0.0 all-gather.4.cloned.1.call-done
  78.5 40.3 %all-gather.6.cloned.1.call-done = bf16[512,2048]{1,0:T(8,128)(2,1)} async-done(((bf16[512,512]{1,0:T(8,128)(2,1)}), bf16[512,2048]{1,0:T(8,128)(2,1)}) %all-gather.6.cloned.1.call-update) | async-done | bytes 2097168 | tf_op jit(solution)/shard_map/all_gather | solution.py:47
  118.8 0.0 copy-start.1
  118.8 3.2 %copy.23 = bf16[2048,512]{1,0:T(8,128)(2,1)} copy(bf16[2048,512]{1,0:T(8,128)(2,1)} %all-gather.4.cloned.1.call-done) | data formatting | bytes 4194304
  122.0 0.8 copy.24
  122.8 0.8 copy.25
  123.6 0.0 copy-done.1
  123.6 1.3 %copy.26 = bf16[512,2048]{1,0:T(8,128)(2,1)} copy(bf16[512,2048]{1,0:T(8,128)(2,1)S(1)} %copy-done.1) | data formatting | bytes 4194304
  (1 shorter events, 0.0 us)
Async XLA Ops:
  7.2 0.8 copy-start
  7.2 5.2 %copy-start.2 = (bf16[512,128]{1,0:T(8,128)(2,1)S(1)}, bf16[512,128]{1,0:T(8,128)(2,1)}, u32[]{:S(2)}) copy-start(bf16[512,128]{1,0:T(8,128)(2,1)} %param.17) | copy-start | bytes 393220
  7.2 5.2 %copy-start.4 = (bf16[512,32]{0,1:T(8,128)(2,1)S(1)}, bf16[512,32]{0,1:T(8,128)(2,1)}, u32[]{:S(2)}) copy-start(bf16[512,32]{0,1:T(8,128)(2,1)} %param.18) | copy-start | bytes 98308
  7.2 5.2 %copy-start.6 = (bf16[32,128]{1,0:T(8,128)(2,1)S(1)}, bf16[32,128]{1,0:T(8,128)(2,1)}, u32[]{:S(2)}) copy-start(bf16[32,128]{1,0:T(8,128)(2,1)} %param.19) | copy-start | bytes 24580
  7.2 28.6 %copy-start.3 = (bf16[512,128]{1,0:T(8,128)(2,1)S(1)}, bf16[512,128]{1,0:T(8,128)(2,1)}, u32[]{:S(2)}) copy-start(bf16[512,128]{1,0:T(8,128)(2,1)} %param.20) | copy-start | bytes 393220
  7.2 28.6 %copy-start.5 = (bf16[512,32]{0,1:T(8,128)(2,1)S(1)}, bf16[512,32]{0,1:T(8,128)(2,1)}, u32[]{:S(2)}) copy-start(bf16[512,32]{0,1:T(8,128)(2,1)} %param.21) | copy-start | bytes 98308
  7.2 28.5 %copy-start.7 = (bf16[32,128]{1,0:T(8,128)(2,1)S(1)}, bf16[32,128]{1,0:T(8,128)(2,1)}, u32[]{:S(2)}) copy-start(bf16[32,128]{1,0:T(8,128)(2,1)} %param.22) | copy-start | bytes 24580
  7.2 71.2 %all-gather.4.cloned.1.call-start = ((), (), s32[]{:S(2)}) async-start(), calls=%async_computation | async-start | bytes 2621440 | tf_op jit(solution)/shard_map/all_gather | solution.py:44
  10.1 47.3 %copy-start.8 = (f32[128]{0:T(128)S(1)}, f32[128]{0:T(128)}, u32[]{:S(2)}) copy-start(f32[128]{0:T(128)} %param.26) | copy-start | bytes 1540
  10.1 47.3 %copy-start.9 = (f32[128]{0:T(128)S(1)}, f32[128]{0:T(128)}, u32[]{:S(2)}) copy-start(f32[128]{0:T(128)} %param.27) | copy-start | bytes 1540
  10.1 108.7 %all-gather.6.cloned.1.call-start = ((), (), s32[]{:S(2)}) async-start(), calls=%async_computation.1 | async-start | bytes 2621440 | tf_op jit(solution)/shard_map/all_gather | solution.py:47
  118.8 4.8 %copy-start.1 = (bf16[512,2048]{1,0:T(8,128)(2,1)S(1)}, bf16[512,2048]{1,0:T(8,128)(2,1)}, u32[]{:S(2)}) copy-start(bf16[512,2048]{1,0:T(8,128)(2,1)} %all-gather.6.cloned.1.call-done) | copy-start | bytes 6291460
Sparse Core Ops, SparseCore 0:
  10.3 60.5 all-gather.3
  73.0 45.7 all-gather.5
where the time goes:
time: 132 us
  blocking collectives  65 us (49%)
  waiting for transfers between devices  40.3 us (31%)
  between operations  14.2 us (11%)
  local copies, waits for them, and re-layouts  6.78 us (5%)
  matrix products  4.8 us (4%)
    all_gather x1, waiting for transfers between devices, shards(): lax.all_gather(narrow_mixed, 'zero', axis=1, tiled=True)  40.3 us
    all_gather x1, blocking collectives, shards(): lax.all_gather(narrow_key, 'zero', axis=0, tiled=True)  23.1 us
    all_gather x1, blocking collectives, shards(): lax.all_gather(narrow_value, 'zero', axis=0, tiled=True)  21.4 us
    all_gather x1, blocking collectives, shards(): lax.all_gather((norm_train + norm_step).astype(jnp.bfloat16), ('zero', 'm...  20.5 us
    unnamed x24, local copies, waits for them, and re-layouts  6.78 us
  transfers between devices with their start and end apart: 2, of which 1 were waited for; matrix products, arithmetic and copies ran while one was open for 2% of the time, Pallas kernels for 0%

commit v1 on v0

--- a/solution.py
+++ b/solution.py
@@ -44,7 +44,7 @@
         lax.all_gather(narrow_query, "zero", axis=0, tiled=True),
         lax.all_gather(narrow_key, "zero", axis=0, tiled=True),
         lax.all_gather(narrow_value, "zero", axis=0, tiled=True),
-        lax.all_gather(narrow_mixed, "zero", axis=1, tiled=True),
+        jnp.concatenate(lax.all_gather(narrow_mixed, "zero"), axis=1),
     )
     serve_norm = lax.all_gather(
         (norm_train + norm_step).astype(jnp.bfloat16), ("zero", "model"), axis=0, tiled=True

time: 132 us -> 131 us (level)
  waiting for transfers between devices: 40.3 us -> 37 us
  local copies, waits for them, and re-layouts: 6.78 us -> 8.64 us
    all_gather x1, waiting for transfers between devices: 40.3 us -> 0.01 us  [shards(): lax.all_gather(narrow_mixed, 'zero')]
    all_gather x1, waiting for transfers between devices: 0.01 us -> 37 us  [shards(): lax.all_gather(narrow_query, 'zero', axis=0, tiled=True)]
    reshape x0 -> x1, local copies, waits for them, and re-layouts: none -> 3.33 us  [shards(): jnp.concatenate(lax.all_gather(narrow_mixed, 'zero'), axis=1)]
    unnamed x24 -> x21, local copies, waits for them, and re-layouts: 6.78 us -> 5.31 us
  transfers between devices with their start and end apart: 2 -> 2, of which waited for: 1 -> 1; matrix products, arithmetic and copies ran while one was open for 2% -> 5% of each run, Pallas kernels for 0% -> 0%
where the time goes in v1:
time: 131 us; the launch traced here: 130 us
  blocking collectives  65 us (50%)
  waiting for transfers between devices  37 us (28%)
  between operations  14.2 us (11%)
  local copies, waits for them, and re-layouts  8.64 us (7%)
  matrix products  4.8 us (4%)
    all_gather x1, waiting for transfers between devices, shards(): lax.all_gather(narrow_query, 'zero', axis=0, tiled=True)  37 us
    all_gather x1, blocking collectives, shards(): lax.all_gather(narrow_key, 'zero', axis=0, tiled=True)  23.1 us
    all_gather x1, blocking collectives, shards(): lax.all_gather(narrow_value, 'zero', axis=0, tiled=True)  21.4 us
    all_gather x1, blocking collectives, shards(): lax.all_gather((norm_train + norm_step).astype(jnp.bfloat16), ('zero', 'm...  20.5 us
    unnamed x21, local copies, waits for them, and re-layouts  5.31 us
    reshape x1, local copies, waits for them, and re-layouts, shards(): jnp.concatenate(lax.all_gather(narrow_mixed, 'zero'), axis=1)  3.33 us
  transfers between devices with their start and end apart: 2, of which 1 were waited for; matrix products, arithmetic and copies ran while one was open for 5% of the time, Pallas kernels for 0%

profile of v1, /device:TPU:0, one launch (start us, length us, event | category | flops | bytes accessed | tf_op | source)
XLA Modules:
  0.0 130.3 jit_solution(15425311209474036477)
XLA Ops:
  7.2 0.0 copy-start
  7.2 0.0 copy-start.1
  7.2 0.0 copy-start.3
  7.2 0.0 copy-start.5
  7.2 0.0 copy-start.2
  7.2 0.0 copy-start.4
  7.2 0.0 copy-start.6
  7.2 0.0 all-gather.7.cloned.1.call-start
  7.3 0.6 copy-done
  7.9 2.2 %fusion.3 = bf16[512,512]{1,0:T(8,128)(2,1)} fusion(bf16[512,32]{0,1:T(8,128)(2,1)S(1)} %copy-done, bf16[32,512]{1,0:T(8,128)(2,1)} %param.25, bf16[512,512]{1,0:T(8,128)(2,1)} %param.23), kind=kOutput, calls=%fused_computation.5 | convolution fusion | flops 17825792 | bytes 1114112 | tf_op jit(solution)/shard_map/dot_general | solution.py:34
  10.1 0.0 copy-start.7
  10.1 0.0 copy-start.8
  10.1 0.0 all-gather.7.cloned.1.call-update
  10.1 0.0 all-gather.5.cloned.1.call-start
  10.2 2.2 %fusion.2 = bf16[512,512]{1,0:T(8,128)(2,1)} fusion(bf16[512,32]{0,1:T(8,128)(2,1)} %param.15, bf16[32,512]{1,0:T(8,128)(2,1)} %param.16, bf16[512,512]{1,0:T(8,128)(2,1)} %param.14), kind=kOutput, calls=%fused_computation.4 | convolution fusion | flops 17825792 | bytes 1114112 | tf_op jit(solution)/shard_map/dot_general | solution.py:25
  12.4 0.0 all-gather.5.cloned.1.call-update
  12.4 0.0 copy-done.1
  12.4 0.0 copy-done.3
  12.4 0.0 copy-done.5
  12.4 0.2 fusion.6
  12.7 23.1 %all_gather.19 = bf16[2048,128]{1,0:T(8,128)(2,1)S(1)} all-gather(bf16[512,128]{1,0:T(8,128)(2,1)S(1)} %fusion.6), channel_id=1, replica_groups=mesh['zero'=4,'model'=4,'trial'=2] {'zero'}, dimensions={0}, use_global_device_ids=true | all-gather | bytes 655360 | tf_op jit(solution)/shard_map/all_gather | solution.py:45
  35.8 0.0 copy-done.2
  35.8 0.0 copy-done.4
  35.8 0.0 copy-done.6
  35.8 0.2 fusion.7
  36.0 21.4 %all_gather.20 = bf16[2048,128]{1,0:T(8,128)(2,1)S(1)} all-gather(bf16[512,128]{1,0:T(8,128)(2,1)S(1)} %fusion.7), channel_id=1, replica_groups=mesh['zero'=4,'model'=4,'trial'=2] {'zero'}, dimensions={0}, use_global_device_ids=true | all-gather | bytes 655360 | tf_op jit(solution)/shard_map/all_gather | solution.py:46
  57.4 0.0 copy-done.7
  57.4 0.0 copy-done.8
  57.4 20.5 %all-gather.1 = bf16[16,1,128]{2,1,0:T(2,128)(2,1)S(1)} all-gather(bf16[1,1,128]{2,1,0:T(2,128)(2,1)S(1)} %convert_bitcast_fusion), channel_id=1, replica_groups=mesh['zero'=4,'model'=4,'trial'=2] {'zero','model'}, dimensions={0}, use_global_device_ids=true | all-gather | bytes 4352 | tf_op jit(solution)/shard_map/all_gather | solution.py:49
  77.9 0.6 reduce
  78.5 0.0 all-gather.7.cloned.1.call-done
  78.5 3.3 %copy.22 = bf16[4,64,8,512]{3,2,0,1:T(8,128)(2,1)} copy(bf16[4,64,8,512]{3,2,1,0:T(8,128)(2,1)} %bitcast.16) | data formatting | bytes 4194304 | tf_op jit(solution)/shard_map/reshape | solution.py:47
  81.8 37.0 %all-gather.5.cloned.1.call-done = bf16[2048,512]{1,0:T(8,128)(2,1)} async-done(((bf16[512,512]{1,0:T(8,128)(2,1)}), bf16[2048,512]{1,0:T(8,128)(2,1)}) %all-gather.5.cloned.1.call-update) | async-done | bytes 2097168 | tf_op jit(solution)/shard_map/all_gather | solution.py:44
  118.8 3.0 %copy.26 = bf16[2048,512]{1,0:T(8,128)(2,1)} copy(bf16[2048,512]{1,0:T(8,128)(2,1)} %all-gather.5.cloned.1.call-done) | data formatting | bytes 4194304
  121.9 0.8 copy.27
  122.6 0.8 copy.28
  (1 shorter events, 0.0 us)
Async XLA Ops:
  7.2 0.8 copy-start
  7.2 5.2 %copy-start.1 = (bf16[512,128]{1,0:T(8,128)(2,1)S(1)}, bf16[512,128]{1,0:T(8,128)(2,1)}, u32[]{:S(2)}) copy-start(bf16[512,128]{1,0:T(8,128)(2,1)} %param.17) | copy-start | bytes 393220
  7.2 5.2 %copy-start.3 = (bf16[512,32]{0,1:T(8,128)(2,1)S(1)}, bf16[512,32]{0,1:T(8,128)(2,1)}, u32[]{:S(2)}) copy-start(bf16[512,32]{0,1:T(8,128)(2,1)} %param.18) | copy-start | bytes 98308
  7.2 5.2 %copy-start.5 = (bf16[32,128]{1,0:T(8,128)(2,1)S(1)}, bf16[32,128]{1,0:T(8,128)(2,1)}, u32[]{:S(2)}) copy-start(bf16[32,128]{1,0:T(8,128)(2,1)} %param.19) | copy-start | bytes 24580
  7.2 28.6 %copy-start.2 = (bf16[512,128]{1,0:T(8,128)(2,1)S(1)}, bf16[512,128]{1,0:T(8,128)(2,1)}, u32[]{:S(2)}) copy-start(bf16[512,128]{1,0:T(8,128)(2,1)} %param.20) | copy-start | bytes 393220
  7.2 28.6 %copy-start.4 = (bf16[512,32]{0,1:T(8,128)(2,1)S(1)}, bf16[512,32]{0,1:T(8,128)(2,1)}, u32[]{:S(2)}) copy-start(bf16[512,32]{0,1:T(8,128)(2,1)} %param.21) | copy-start | bytes 98308
  7.2 28.5 %copy-start.6 = (bf16[32,128]{1,0:T(8,128)(2,1)S(1)}, bf16[32,128]{1,0:T(8,128)(2,1)}, u32[]{:S(2)}) copy-start(bf16[32,128]{1,0:T(8,128)(2,1)} %param.22) | copy-start | bytes 24580
  7.2 71.3 %all-gather.7.cloned.1.call-start = ((), (), s32[]{:S(2)}) async-start(), calls=%async_computation.1 | async-start | bytes 2621440 | tf_op jit(solution)/shard_map/all_gather | solution.py:47
  10.1 47.3 %copy-start.7 = (f32[128]{0:T(128)S(1)}, f32[128]{0:T(128)}, u32[]{:S(2)}) copy-start(f32[128]{0:T(128)} %param.26) | copy-start | bytes 1540
  10.1 47.3 %copy-start.8 = (f32[128]{0:T(128)S(1)}, f32[128]{0:T(128)}, u32[]{:S(2)}) copy-start(f32[128]{0:T(128)} %param.27) | copy-start | bytes 1540
  10.1 108.7 %all-gather.5.cloned.1.call-start = ((), (), s32[]{:S(2)}) async-start(), calls=%async_computation | async-start | bytes 2621440 | tf_op jit(solution)/shard_map/all_gather | solution.py:44
Sparse Core Ops, SparseCore 0:
  10.3 60.5 all-gather.6
  73.0 45.7 all-gather.4
